TPU v7x, 128 devices: a whole 4x4x4 slice. The times are simulated.
128 devices in a mesh: seq: 32 (over z, x, core), mp: 4 (over y).
Axes of the slice: x: 4, y: 4, z: 4, core: 2. Of those that a mesh axis runs over, the one named last changes fastest.
Arguments:
- teacher_query: bfloat16 [5120, 8192], P('seq', 'mp'), may hold values from -37 to 37
- teacher_keys: bfloat16 [5120, 1024], P('seq', 'mp'), may hold values from -4 to 4
- teacher_values: bfloat16 [5120, 1024], P('seq', 'mp'), may hold values from -4 to 4
- teacher_docs: int32 [16], replicated, may hold values from 1 to 3840, 5120 in all
- student_query: bfloat16 [5120, 3584], P('seq', 'mp'), may hold values from -37 to 37
- student_keys: bfloat16 [5120, 512], P('seq', 'mp'), may hold values from -4 to 4
- student_values: bfloat16 [5120, 512], P('seq', 'mp'), may hold values from -4 to 4
- student_docs: int32 [16], replicated, may hold values from 1 to 3840, 5120 in all
- projector: bfloat16 [8192, 3584], P('mp'), may hold values from -0.125 to 0.125
- teacher_spans: int32 [32, 2, 128], P('seq'), may hold values from 0 to 159, as said below
- student_spans: int32 [32, 2, 128], P('seq'), may hold values from 0 to 159, as said below
Outputs:
- grad_query: bfloat16 [5120, 3584], P('seq', 'mp')
- grad_keys: bfloat16 [5120, 512], P('seq', 'mp')
- grad_values: bfloat16 [5120, 512], P('seq', 'mp')
Inputs may be any that keep to these rules, and one draw needn't show every extreme that they name: `teacher_spans`: column d * 4 + c of row r holds, first, the first teacher position of a span (counted within the 160 positions of index r along seq) and, second, its number of positions; it is the c-th span that index r sends to index d. A count of 0 marks an empty slot; the live slots of one destination come first; live spans cover 1 to 4 positions inside the index's positions and may intersect. One source sends at most 4 spans to one destination, and in every draw some destination receives 4 from every source. `student_spans`: column r * 4 + c of row d holds the student range (first position within the 160 positions of index d along seq, then the number of positions) of the span in column d * 4 + c of row r of teacher_spans; the count is 0 exactly where that teacher slot is empty, else 1 to 4. Ranges may intersect.
All inputs are finite; a program needn't handle non-finite values.
Results may differ from a plain program's by a relative error of at most 0.015.
Values may be sent and summed in bfloat16 or wider, within the bound.
A program may use at most 128 MiB of HBM per device.

v0:
```python
import jax
import jax.numpy as jnp
from jax import lax
from jax.sharding import PartitionSpec as P

HD = 128
NEG = -1e30


def sent_together(arrays, axis, dim, along):
    ends, at = ([], 0)
    for a in arrays[:-1]:
        at += a.shape[along]
        ends.append(at)
    both = jnp.concatenate(arrays, axis=along)
    return tuple(jnp.split(lax.all_gather(both, axis, axis=dim, tiled=True), ends, axis=along))


def doc_index(lengths, positions):
    bounds = jnp.cumsum(lengths)
    return jnp.sum((bounds[None, :] <= positions[:, None]).astype(jnp.int32), axis=1)


def block_size(total_rows):
    size_now = min(512, total_rows)
    while total_rows % size_now:
        size_now -= 1
    return size_now


def keep_same(carried):
    return carried


def allowed_pairs(query_docs, query_places, docs, key_places):
    same_doc = doc_index(docs, key_places)[None, :] == query_docs[:, None]
    return same_doc & (key_places[None, :] <= query_places[:, None])


def members(spans, tok_rows):
    starts = spans[0, 0]
    lengths = spans[0, 1]
    places = jnp.arange(tok_rows, dtype=jnp.int32)
    inside = (places[None, :] >= starts[:, None]) & (places[None, :] < (starts + lengths)[:, None])
    return (inside.astype(jnp.bfloat16), 1.0 / jnp.maximum(lengths, 1).astype(jnp.float32))


def empty_state(tok_rows, groups_here, head_ratio):
    return (
        jnp.full((groups_here, head_ratio, tok_rows), NEG, jnp.float32),
        jnp.zeros((groups_here, head_ratio, tok_rows), jnp.float32),
        jnp.zeros((groups_here, head_ratio, tok_rows, HD), jnp.float32),
    )


def attend_block(running, queries, key_block, value_block, allowed, score_scale):
    row_peak, totals, weighted = running
    scores = (
        jnp.einsum("qgrd,kgd->grqk", queries, key_block, preferred_element_type=jnp.float32)
        * score_scale
    )
    scores = jnp.where(allowed[None, None], scores, NEG)
    new_peak = jnp.maximum(row_peak, jnp.max(scores, axis=-1))
    weights = jnp.where(allowed[None, None], jnp.exp(scores - new_peak[..., None]), 0.0)
    factor = jnp.exp(row_peak - new_peak)
    totals = totals * factor + jnp.sum(weights, axis=-1)
    contrib = jnp.einsum(
        "grqk,kgd->grqd",
        weights.astype(jnp.bfloat16),
        value_block,
        preferred_element_type=jnp.float32,
    )
    return (new_peak, totals, weighted * factor[..., None] + contrib)


def fold_attention(running, queries, key_rows, value_rows, query_docs, query_places, docs):
    piece_rows = key_rows.shape[0]
    groups_here = queries.shape[1]
    step_rows = block_size(piece_rows)
    count_blocks = piece_rows // step_rows
    key_blocks = key_rows.reshape(count_blocks, step_rows, groups_here, HD)
    value_blocks = value_rows.reshape(count_blocks, step_rows, groups_here, HD)
    score_scale = HD ** (-0.5)

    def one_step(carried, inputs):
        number, key_block, value_block = inputs
        key_places = number * step_rows + jnp.arange(step_rows, dtype=jnp.int32)
        allowed = allowed_pairs(query_docs, query_places, docs, key_places)

        def compute(current):
            return attend_block(current, queries, key_block, value_block, allowed, score_scale)

        return (lax.cond(jnp.any(allowed), compute, keep_same, carried), None)

    result, unused = lax.scan(
        one_step, running, (jnp.arange(count_blocks, dtype=jnp.int32), key_blocks, value_blocks)
    )
    return result


def finish(running, tok_rows):
    row_peak, totals, weighted = (running[0], running[1], running[2])
    context = weighted / totals[..., None]
    context = jnp.transpose(context, (2, 0, 1, 3)).reshape(tok_rows, -1).astype(jnp.bfloat16)
    log_sums = jnp.transpose(row_peak + jnp.log(totals), (2, 0, 1)).reshape(tok_rows, -1)
    return (context, log_sums)


def backward_block(
    queries, douts, sums_here, deltas_here, key_block, value_block, allowed, score_scale
):
    scores = (
        jnp.einsum("qgrd,kgd->grqk", queries, key_block, preferred_element_type=jnp.float32)
        * score_scale
    )
    probs = jnp.where(allowed[None, None], jnp.exp(scores - sums_here[..., None]), 0.0)
    prob_grad = jnp.einsum("qgrd,kgd->grqk", douts, value_block, preferred_element_type=jnp.float32)
    dscore = (probs * (prob_grad - deltas_here[..., None])).astype(jnp.bfloat16)
    return (probs.astype(jnp.bfloat16), dscore)


def key_term(probs_low, dscore, queries, douts, score_scale):
    key_grad = (
        jnp.einsum("grqk,qgrd->kgd", dscore, queries, preferred_element_type=jnp.float32)
        * score_scale
    )
    value_grad = jnp.einsum("grqk,qgrd->kgd", probs_low, douts, preferred_element_type=jnp.float32)
    rows_here = key_grad.shape[0]
    return jnp.concatenate(
        [key_grad.reshape(rows_here, -1), value_grad.reshape(rows_here, -1)], axis=1
    )


def fold_grads(
    running,
    queries,
    douts,
    sums_here,
    deltas_here,
    query_docs,
    query_places,
    docs,
    key_rows,
    value_rows,
):
    piece_rows = key_rows.shape[0]
    groups_here = queries.shape[1]
    step_rows = block_size(piece_rows)
    count_blocks = piece_rows // step_rows
    key_blocks = key_rows.reshape(count_blocks, step_rows, groups_here, HD)
    value_blocks = value_rows.reshape(count_blocks, step_rows, groups_here, HD)
    score_scale = HD ** (-0.5)
    term_width = 2 * groups_here * HD

    def one_step(carried, inputs):
        number, key_block, value_block = inputs
        key_places = number * step_rows + jnp.arange(step_rows, dtype=jnp.int32)
        allowed = allowed_pairs(query_docs, query_places, docs, key_places)

        def compute(current):
            probs_low, dscore = backward_block(
                queries, douts, sums_here, deltas_here, key_block, value_block, allowed, score_scale
            )
            updated = (
                current
                + jnp.einsum(
                    "grqk,kgd->qgrd", dscore, key_block, preferred_element_type=jnp.float32
                )
                * score_scale
            )
            return (updated, key_term(probs_low, dscore, queries, douts, score_scale))

        def passing(current):
            return (current, jnp.zeros((step_rows, term_width), jnp.float32))

        return lax.cond(jnp.any(allowed), compute, passing, carried)

    grad_query, terms = lax.scan(
        one_step, running[0], (jnp.arange(count_blocks, dtype=jnp.int32), key_blocks, value_blocks)
    )
    key_terms = terms.reshape(piece_rows, term_width)
    return (grad_query, key_terms)


def body(
    teacher_query,
    teacher_keys,
    teacher_values,
    teacher_docs,
    student_query,
    student_keys,
    student_values,
    student_docs,
    projector,
    teacher_spans,
    student_spans,
):
    tok_rows = teacher_query.shape[0]
    all_rows = tok_rows * lax.axis_size("seq")
    teacher_groups = teacher_keys.shape[1] // HD
    teacher_ratio = teacher_query.shape[1] // HD // teacher_groups
    student_groups = student_keys.shape[1] // HD
    student_ratio = student_query.shape[1] // HD // student_groups
    query_places = lax.axis_index("seq") * tok_rows + jnp.arange(tok_rows, dtype=jnp.int32)
    teacher_qdocs = doc_index(teacher_docs, query_places)
    student_qdocs = doc_index(student_docs, query_places)
    teacher_q = teacher_query.reshape(tok_rows, teacher_groups, teacher_ratio, HD)
    student_q = student_query.reshape(tok_rows, student_groups, student_ratio, HD)
    teacher_init = empty_state(tok_rows, teacher_groups, teacher_ratio)
    student_init = empty_state(tok_rows, student_groups, student_ratio)
    pieces = (
        lax.all_gather(teacher_keys, "seq", axis=0, tiled=True),
        lax.all_gather(teacher_values, "seq", axis=0, tiled=True),
    )
    teacher_state = fold_attention(
        teacher_init, teacher_q, pieces[0], pieces[1], teacher_qdocs, query_places, teacher_docs
    )
    pieces = (
        lax.all_gather(student_keys, "seq", axis=0, tiled=True),
        lax.all_gather(student_values, "seq", axis=0, tiled=True),
    )
    attended = fold_attention(
        student_init[:3], student_q, pieces[0], pieces[1], student_qdocs, query_places, student_docs
    )
    student_state = tuple(attended)
    teacher_context, unused = finish(teacher_state, tok_rows)
    member_teacher, weight_teacher = members(teacher_spans, tok_rows)
    pooled_teacher = (
        jnp.dot(member_teacher, teacher_context, preferred_element_type=jnp.float32)
        * weight_teacher[:, None]
    ).astype(jnp.bfloat16)
    projected = jnp.dot(pooled_teacher, projector, preferred_element_type=jnp.float32)
    targets = lax.psum_scatter(
        projected.astype(jnp.bfloat16), "mp", scatter_dimension=1, tiled=True
    )
    arrived = lax.all_to_all(targets, "seq", split_axis=0, concat_axis=0, tiled=True)
    student_context, student_sums = finish(student_state, tok_rows)
    member_student, weight_student = members(student_spans, tok_rows)
    pooled_student = (
        jnp.dot(member_student, student_context, preferred_element_type=jnp.float32)
        * weight_student[:, None]
    )
    live_rows = (student_spans[0, 1] > 0)[:, None]
    residual = (
        jnp.where(live_rows, pooled_student - arrived.astype(jnp.float32), 0.0)
        * weight_student[:, None]
    )
    grad_out = jnp.dot(jnp.transpose(member_student.astype(jnp.float32)), residual).astype(
        jnp.bfloat16
    )
    heads_here = student_groups * student_ratio
    deltas = jnp.sum(
        (grad_out.astype(jnp.float32) * student_context.astype(jnp.float32)).reshape(
            tok_rows, heads_here, HD
        ),
        axis=-1,
    )
    student_dout = grad_out.reshape(tok_rows, student_groups, student_ratio, HD)
    sums_here = jnp.transpose(
        student_sums.reshape(tok_rows, student_groups, student_ratio), (1, 2, 0)
    )
    deltas_here = jnp.transpose(deltas.reshape(tok_rows, student_groups, student_ratio), (1, 2, 0))
    term_width = 2 * student_keys.shape[1]
    grad_init = (jnp.zeros((tok_rows, student_groups, student_ratio, HD), jnp.float32),)
    grad_init = grad_init + (jnp.zeros((all_rows, term_width), jnp.float32),)
    pieces = sent_together((student_keys, student_values), "seq", 0, 1)
    grad_state = fold_grads(
        grad_init,
        student_q,
        student_dout,
        sums_here,
        deltas_here,
        student_qdocs,
        query_places,
        student_docs,
        pieces[0],
        pieces[1],
    )
    grad_query = grad_state[0].reshape(tok_rows, -1).astype(jnp.bfloat16)
    key_terms = lax.psum_scatter(
        grad_state[1].astype(jnp.bfloat16), "seq", scatter_dimension=0, tiled=True
    ).astype(jnp.float32)
    half_width = student_keys.shape[1]
    return (
        grad_query,
        key_terms[:, :half_width].astype(jnp.bfloat16),
        key_terms[:, half_width:].astype(jnp.bfloat16),
    )


def solution(mesh):
    return jax.shard_map(
        body,
        mesh=mesh,
        in_specs=(
            P("seq", "mp"),
            P("seq", "mp"),
            P("seq", "mp"),
            P(),
            P("seq", "mp"),
            P("seq", "mp"),
            P("seq", "mp"),
            P(),
            P("mp", None),
            P("seq", None, None),
            P("seq", None, None),
        ),
        out_specs=(P("seq", "mp"), P("seq", "mp"), P("seq", "mp")),
        check_vma=False,
    )
```

profile of v0, /device:TPU:0, one launch (start us, length us, event | category | flops | bytes accessed | tf_op | source)
XLA Modules:
  0.0 442.9 jit_solution(18287715508610465166)
XLA Ops:
  12.1 0.8 broadcast_in_dim.162
  13.0 0.8 broadcast_in_dim.170
  13.8 1.2 copy.55
  15.3 41.9 %all-gather.12.cloned.1.call-done = bf16[5120,256]{1,0:T(8,128)(2,1)} async-done(((bf16[160,256]{1,0:T(8,128)(2,1)}), bf16[5120,256]{1,0:T(8,128)(2,1)}) %all-gather.12.cloned.1.call-update) | async-done | bytes 2621456 | tf_op jit(solution)/shard_map/all_gather | solution.py:212
  57.2 3.5 reshape.307
  60.8 2.1 copy.41
  62.8 40.4 %all-gather.14.cloned.1.call-done = bf16[5120,256]{1,0:T(8,128)(2,1)} async-done(((bf16[160,256]{1,0:T(8,128)(2,1)}), bf16[5120,256]{1,0:T(8,128)(2,1)}) %all-gather.14.cloned.1.call-update) | async-done | bytes 2621456 | tf_op jit(solution)/shard_map/all_gather | solution.py:213
  103.2 3.5 reshape.309
  106.8 2.0 copy.43
  109.0 35.1 %while.53 = (s32[]{:T(128)}, f32[2,8,160]{2,1,0:T(8,128)S(1)}, f32[2,8,160]{2,1,0:T(8,128)S(1)}, f32[2,8,160,128]{3,2,1,0:T(8,128)S(1)}, s32[1,16]{1,0:T(1,128)S...) while((s32[]{:T(128)}, f32[2,8,160]{2,1,0:T(8,128)S(1)}, ...), condition=%wide.region_19.20_spmd.clone, body=%wide.region_12.19_spmd.clone.sunk | while | flops 689140928 | bytes 20034780 | solution.py:95
  110.3 0.8 fusion.135
  111.8 7.0 %conditional.10 = ((f32[2,8,160]{2,1,0:T(8,128)S(1)}, f32[2,8,160]{2,1,0:T(8,128)S(1)}, f32[2,8,160,128]{3,2,1,0:T(8,128)S(1)})) conditional(s32[]{:T(128)} %convert_element_type.203, (f32[2,8,160]{2,1,0:T(8,128)S(1)}, f32[2,8,160]{2,1,0:T(8,128)S(1)}, f32[2,8,160,128]{3,2,1,0:T(8,128)S(1)}) %tuple.156, (pred[160,512]{1,0:T(8,128)(4,1)S(1)}, ...), branch_computations={%region_15.15_spmd, %region_16.18_spmd} | conditional | flops 688788480 | bytes 19940384 | solution.py:93
  111.8 2.0 fusion.29
  113.8 1.9 fusion.31
  115.7 3.1 fusion.35
  120.1 0.8 fusion.135
  122.9 0.8 fusion.135
  125.7 0.8 fusion.135
  128.5 0.8 fusion.135
  131.3 0.8 fusion.135
  134.1 0.8 fusion.135
  137.0 0.8 fusion.135
  139.8 0.8 fusion.135
  142.6 0.8 fusion.135
  144.7 7.5 %convolution_convert_fusion = bf16[128,3584]{1,0:T(8,128)(2,1)S(1)} fusion(bf16[2048,3584]{1,0:T(8,128)(2,1)} %param.31, bf16[20,8,16,128]{3,2,1,0:T(8,128)(2,1)S(1)} %bitcast.238, f32[128]{0:T(128)S(1)} %fusion.114, s32[128]{0:T(128)S(1)} %bitcast_add_fusion.1, s32[128]{0:T(128)S(1)} %slice_bitcast_fusion), kind=kOutput, calls=%fused_computation.100 | convolution fusion | flops 1963978752 | bytes 16254464 | tf_op jit(solution)/shard_map/dot_general | solution.py:232
  152.2 1.3 copy.52
  155.0 36.9 %all-gather.10.cloned.1.call-done = bf16[5120,128]{1,0:T(8,128)(2,1)} async-done(((bf16[160,128]{1,0:T(8,128)(2,1)}), bf16[5120,128]{1,0:T(8,128)(2,1)}) %all-gather.10.cloned.1.call-update) | async-done | bytes 1310736 | tf_op jit(solution)/shard_map/all_gather | solution.py:220
  192.0 32.4 %while.52 = (s32[]{:T(128)}, f32[1,7,160]{2,1,0:T(8,128)S(1)}, f32[1,7,160]{2,1,0:T(8,128)S(1)}, f32[1,7,160,128]{3,2,1,0:T(8,128)S(1)}, s32[1,16]{1,0:T(1,128)S...) while((s32[]{:T(128)}, f32[1,7,160]{2,1,0:T(8,128)S(1)}, ...), condition=%wide.region_9.10_spmd.clone, body=%wide.region_2.9_spmd.clone.sunk | while | flops 301698496 | bytes 8989915 | solution.py:95
  193.3 0.8 fusion.134
  194.8 4.3 conditional.9
  194.8 1.5 fusion.6
  196.3 1.9 fusion.9
  198.2 0.9 fusion.8
  200.5 0.8 fusion.134
  203.3 0.8 fusion.134
  206.1 0.8 fusion.134
  208.9 0.8 fusion.134
  211.7 0.8 fusion.134
  214.5 0.8 fusion.134
  217.3 0.8 fusion.134
  220.2 0.8 fusion.134
  223.0 0.8 fusion.134
  224.8 5.7 %reduce-scatter.7.cloned.1.call-done = bf16[896,128]{1,0:T(8,128)(2,1)} async-done(((bf16[3584,128]{1,0:T(8,128)(2,1)}), bf16[896,128]{1,0:T(8,128)(2,1)}) %reduce-scatter.7.cloned.1.call-update) | async-done | bytes 229392
  230.5 1.1 copy.53
  232.3 42.8 %all-to-all-start = ((bf16[32,4,896]{2,1,0:T(4,128)(2,1)}), bf16[32,4,896]{2,1,0:T(4,128)(2,1)S(1)}, u32[]{:S(2)}, u32[]{:S(2)}) async-start(bf16[32,4,896]{2,1,0:T(4,128)(2,1)} %all_to_all.6), calls=%async_computation | async-start | bytes 458752 | tf_op jit(solution)/shard_map/all_to_all | solution.py:236
  275.2 1.6 all-gather.6.cloned.1.call-done
  276.8 3.0 fusion.121
  279.8 3.8 all-to-all-done
  285.0 39.6 %while.54 = (s32[]{:T(128)}, f32[160,1,7,128]{3,0,2,1:T(8,128)S(1)}, bf16[10,512,256]{1,2,0:T(8,128)(2,1)}, s32[1,16]{1,0:T(1,128)S(1)}, s32[10]{0:T(128)S(1)}, ...) while((s32[]{:T(128)}, ...), condition=%wide.region_27.28_spmd.clone, body=%wide.region_22.27_spmd.clone.sunk | while | flops 741032128 | bytes 14592339 | solution.py:178
  286.3 0.8 fusion.136
  287.8 4.0 conditional.11
  288.3 1.8 fusion.53
  293.9 0.8 fusion.136
  297.4 0.8 fusion.136
  301.0 0.8 fusion.136
  304.5 0.8 fusion.136
  308.1 0.8 fusion.136
  311.7 0.8 fusion.136
  315.2 0.8 fusion.136
  318.8 0.8 fusion.136
  322.3 0.8 fusion.136
  324.5 4.4 copy.49
  329.9 104.8 %reduce-scatter.5.cloned.1.call-done = bf16[160,256]{1,0:T(8,128)(2,1)} async-done(((bf16[5120,256]{1,0:T(8,128)(2,1)}), bf16[160,256]{1,0:T(8,128)(2,1)}) %reduce-scatter.5.cloned.1.call-update) | async-done | bytes 81936 | tf_op jit(solution)/shard_map/reduce_scatter | solution.py:280
  434.6 1.4 fusion.122
  (240 shorter events, 41.6 us)
Async XLA Ops:
  7.2 50.0 %all-gather.12.cloned.1.call-start = ((), (), s32[]{:S(2)}) async-start(), calls=%async_computation.6 | async-start | bytes 2703360 | tf_op jit(solution)/shard_map/all_gather | solution.py:212
  7.9 95.3 %all-gather.14.cloned.1.call-start = ((), (), s32[]{:S(2)}) async-start(), calls=%async_computation.7 | async-start | bytes 2703360 | tf_op jit(solution)/shard_map/all_gather | solution.py:213
  8.6 146.3 %all-gather.8.cloned.1.call-start = ((), (), s32[]{:S(2)}) async-start(), calls=%async_computation.4 | async-start | bytes 1351680 | tf_op jit(solution)/shard_map/all_gather | solution.py:219
  9.4 182.5 %all-gather.10.cloned.1.call-start = ((), (), s32[]{:S(2)}) async-start(), calls=%async_computation.5 | async-start | bytes 1351680 | tf_op jit(solution)/shard_map/all_gather | solution.py:220
  10.0 220.5 %reduce-scatter.7.cloned.1.call-start = ((), (), s32[]{:S(2)}) async-start(), calls=%async_computation.9 | async-start | bytes 1146880
  152.2 1.6 copy-start.1
  152.2 1.6 copy-start.2
  152.2 2.3 copy-start.3
  152.2 2.3 copy-start
  153.6 123.2 %all-gather.6.cloned.1.call-start = ((), (), s32[]{:S(2)}) async-start(), calls=%async_computation.3 | async-start | bytes 2703360 | tf_op jit(solution)/shard_map/all_gather | solution.py:16
  232.3 51.3 %all-to-all-start = ((bf16[32,4,896]{2,1,0:T(4,128)(2,1)}), bf16[32,4,896]{2,1,0:T(4,128)(2,1)S(1)}, u32[]{:S(2)}, u32[]{:S(2)}) async-start(bf16[32,4,896]{2,1,0:T(4,128)(2,1)} %all_to_all.6), calls=%async_computation | async-start | bytes 458752 | tf_op jit(solution)/shard_map/all_to_all | solution.py:236
  275.2 159.5 %reduce-scatter.5.cloned.1.call-start = ((), (), s32[]{:S(2)}) async-start(), calls=%async_computation.8 | async-start | bytes 2703360 | tf_op jit(solution)/shard_map/reduce_scatter | solution.py:280
Sparse Core Ops, SparseCore 0:
  10.2 46.9 all-gather.11
  59.5 43.7 all-gather.13
  105.5 42.1 all-gather.7
  149.8 42.1 all-gather.9
  194.2 36.2 reduce-scatter.6
  232.6 44.1 all-gather.5
  329.1 105.5 reduce-scatter.4
where the time goes:
time: 445 us; the launch traced here: 443 us
  waiting for transfers between devices  238 us (53%)
  local copies, waits for them, and re-layouts  52.7 us (12%)
  starting transfers between devices  43.3 us (10%)
  loops' own time  40.6 us (9%)
  other arithmetic  33.8 us (8%)
  matrix products  20.3 us (5%)
  between operations  14.5 us (3%)
    reduce_scatter x1, waiting for transfers between devices, body(): lax.psum_scatter(grad_state[1].astype(jnp.bfloat16), 'seq', scatter_dimen...  105 us
    all_to_all x1, starting transfers between devices, body(): lax.all_to_all(targets, 'seq', split_axis=0, concat_axis=0, tiled=True)  42.8 us
    all_gather x1, waiting for transfers between devices, body(): lax.all_gather(teacher_keys, 'seq', axis=0, tiled=True)  41.9 us
    all_gather x1, waiting for transfers between devices, body(): lax.all_gather(teacher_values, 'seq', axis=0, tiled=True)  40.4 us
    all_gather x1, waiting for transfers between devices, body(): lax.all_gather(student_values, 'seq', axis=0, tiled=True)  36.9 us
    another operation x2, loops' own time, fold_attention(): lax.scan(one_step, running, (jnp.arange(count_blocks, dtype=jnp.int32), k...  26.8 us
    dynamic_slice x30, local copies, waits for them, and re-layouts, fold_attention(): lax.scan(one_step, running, (jnp.arange(count_blocks, dtype=jnp.int32), k...  17.6 us
    reduce_or x20, other arithmetic, one_step(): return (lax.cond(jnp.any(allowed), compute, keep_same, carried), None)  15.6 us
  transfers between devices with their start and end apart: 8, of which 7 were waited for; matrix products, arithmetic and copies ran while one was open for 16% of the time, Pallas kernels for 0%

commit v1 on v0

--- a/solution.py
+++ b/solution.py
@@ -217,7 +217,9 @@
     )
     pieces = (
         lax.all_gather(student_keys, "seq", axis=0, tiled=True),
-        lax.all_gather(student_values, "seq", axis=0, tiled=True),
+        jnp.concatenate(
+            lax.all_to_all(jnp.stack([student_values] * lax.axis_size("seq")), "seq", 0, 0), axis=0
+        ),
     )
     attended = fold_attention(
         student_init[:3], student_q, pieces[0], pieces[1], student_qdocs, query_places, student_docs

time: 445 us -> 466 us (1.047)
  starting transfers between devices: 43.3 us -> 87 us
  waiting for transfers between devices: 238 us -> 214 us
    all_to_all x0 -> x1, starting transfers between devices: none -> 59.7 us  [body(): lax.all_to_all(jnp.stack([student_values] * lax.axis_size('seq')), 'seq',...]
    all_gather x1 -> x0, waiting for transfers between devices: 36.9 us -> none  [body(): lax.all_gather(student_values, 'seq', axis=0, tiled=True)]
    all_to_all x0 -> x1, waiting for transfers between devices: none -> 19.2 us  [body(): lax.all_to_all(jnp.stack([student_values] * lax.axis_size('seq')), 'seq',...]
    all_to_all x1, starting transfers between devices: 42.8 us -> 27 us  [body(): lax.all_to_all(targets, 'seq', split_axis=0, concat_axis=0, tiled=True)]
    unnamed x8 -> x7, waiting for transfers between devices: 8.29 us -> 2.13 us
  transfers between devices with their start and end apart: 8 -> 8, of which waited for: 7 -> 5; matrix products, arithmetic and copies ran while one was open for 16% -> 16% of each run, Pallas kernels for 0% -> 0%
where the time goes in v1:
time: 466 us; the launch traced here: 464 us
  waiting for transfers between devices  214 us (46%)
  starting transfers between devices  87 us (19%)
  local copies, waits for them, and re-layouts  54 us (12%)
  loops' own time  40.6 us (9%)
  other arithmetic  33.8 us (7%)
  matrix products  19.5 us (4%)
  between operations  14.5 us (3%)
    reduce_scatter x1, waiting for transfers between devices, body(): lax.psum_scatter(grad_state[1].astype(jnp.bfloat16), 'seq', scatter_dimen...  105 us
    all_to_all x1, starting transfers between devices, body(): lax.all_to_all(jnp.stack([student_values] * lax.axis_size('seq')), 'seq',...  59.7 us
    all_gather x1, waiting for transfers between devices, body(): lax.all_gather(teacher_keys, 'seq', axis=0, tiled=True)  42.5 us
    all_gather x1, waiting for transfers between devices, body(): lax.all_gather(teacher_values, 'seq', axis=0, tiled=True)  40.4 us
    all_to_all x1, starting transfers between devices, body(): lax.all_to_all(targets, 'seq', split_axis=0, concat_axis=0, tiled=True)  27 us
    another operation x2, loops' own time, fold_attention(): lax.scan(one_step, running, (jnp.arange(count_blocks, dtype=jnp.int32), k...  26.7 us
    all_to_all x1, waiting for transfers between devices, body(): lax.all_to_all(jnp.stack([student_values] * lax.axis_size('seq')), 'seq',...  19.2 us
    dynamic_slice x30, local copies, waits for them, and re-layouts, fold_attention(): lax.scan(one_step, running, (jnp.arange(count_blocks, dtype=jnp.int32), k...  17.6 us
  transfers between devices with their start and end apart: 8, of which 5 were waited for; matrix products, arithmetic and copies ran while one was open for 16% of the time, Pallas kernels for 0%

profile of v1, /device:TPU:0, one launch (start us, length us, event | category | flops | bytes accessed | tf_op | source)
XLA Modules:
  0.0 463.6 jit_solution(7219880477021088736)
XLA Ops:
  11.6 0.8 broadcast_in_dim.162
  12.4 0.8 broadcast_in_dim.170
  13.2 1.2 copy.55
  14.7 42.5 %all-gather.9.cloned.1.call-done = bf16[5120,256]{1,0:T(8,128)(2,1)} async-done(((bf16[160,256]{1,0:T(8,128)(2,1)}), bf16[5120,256]{1,0:T(8,128)(2,1)}) %all-gather.9.cloned.1.call-update) | async-done | bytes 2621456 | tf_op jit(solution)/shard_map/all_gather | solution.py:212
  57.2 3.5 reshape.305
  60.8 2.1 copy.41
  62.8 40.4 %all-gather.11.cloned.1.call-done = bf16[5120,256]{1,0:T(8,128)(2,1)} async-done(((bf16[160,256]{1,0:T(8,128)(2,1)}), bf16[5120,256]{1,0:T(8,128)(2,1)}) %all-gather.11.cloned.1.call-update) | async-done | bytes 2621456 | tf_op jit(solution)/shard_map/all_gather | solution.py:213
  103.2 3.5 reshape.307
  106.8 2.0 copy.43
  109.0 35.1 %while.53 = (s32[]{:T(128)}, f32[2,8,160]{2,1,0:T(8,128)S(1)}, f32[2,8,160]{2,1,0:T(8,128)S(1)}, f32[2,8,160,128]{3,2,1,0:T(8,128)S(1)}, s32[1,16]{1,0:T(1,128)S...) while((s32[]{:T(128)}, f32[2,8,160]{2,1,0:T(8,128)S(1)}, ...), condition=%wide.region_19.20_spmd.clone, body=%wide.region_12.19_spmd.clone.sunk | while | flops 689140928 | bytes 20034780 | solution.py:95
  110.3 0.8 fusion.135
  111.8 7.0 %conditional.10 = ((f32[2,8,160]{2,1,0:T(8,128)S(1)}, f32[2,8,160]{2,1,0:T(8,128)S(1)}, f32[2,8,160,128]{3,2,1,0:T(8,128)S(1)})) conditional(s32[]{:T(128)} %convert_element_type.203, (f32[2,8,160]{2,1,0:T(8,128)S(1)}, f32[2,8,160]{2,1,0:T(8,128)S(1)}, f32[2,8,160,128]{3,2,1,0:T(8,128)S(1)}) %tuple.156, (pred[160,512]{1,0:T(8,128)(4,1)S(1)}, ...), branch_computations={%region_15.15_spmd, %region_16.18_spmd} | conditional | flops 688788480 | bytes 19940384 | solution.py:93
  111.8 2.0 fusion.29
  113.8 1.9 fusion.31
  115.7 3.1 fusion.35
  120.1 0.8 fusion.135
  122.9 0.8 fusion.135
  125.7 0.8 fusion.135
  128.5 0.8 fusion.135
  131.3 0.8 fusion.135
  134.1 0.8 fusion.135
  137.0 0.8 fusion.135
  139.8 0.8 fusion.135
  142.6 0.8 fusion.135
  144.7 7.5 %convolution_convert_fusion = bf16[128,3584]{1,0:T(8,128)(2,1)S(1)} fusion(bf16[2048,3584]{1,0:T(8,128)(2,1)} %param.31, bf16[20,8,16,128]{3,2,1,0:T(8,128)(2,1)S(1)} %bitcast.238, f32[128]{0:T(128)S(1)} %fusion.114, s32[128]{0:T(128)S(1)} %bitcast_add_fusion.1, s32[128]{0:T(128)S(1)} %slice_bitcast_fusion), kind=kOutput, calls=%fused_computation.100 | convolution fusion | flops 1963978752 | bytes 16254464 | tf_op jit(solution)/shard_map/dot_general | solution.py:234
  152.2 1.3 copy.52
  153.6 1.2 stack.2
  154.8 59.7 %all-to-all-start = ((bf16[32,160,128]{2,1,0:T(8,128)(2,1)}), bf16[32,160,128]{2,1,0:T(8,128)(2,1)S(1)}, u32[]{:S(2)}, u32[]{:S(2)}) async-start(bf16[32,160,128]{2,1,0:T(8,128)(2,1)} %stack.2), calls=%async_computation | async-start | bytes 2621440 | tf_op jit(solution)/shard_map/all_to_all | solution.py:221
  215.8 19.2 %all-to-all-done = bf16[32,160,128]{2,1,0:T(8,128)(2,1)S(1)} async-done(((bf16[32,160,128]{2,1,0:T(8,128)(2,1)}), bf16[32,160,128]{2,1,0:T(8,128)(2,1)S(1)}, u32[]{:S(2)}, u32[]{:S(2)}) %all-to-all-start) | async-done | bytes 1310752 | tf_op jit(solution)/shard_map/all_to_all | solution.py:221
  235.1 31.5 %while.52 = (s32[]{:T(128)}, f32[1,7,160]{2,1,0:T(8,128)S(1)}, f32[1,7,160]{2,1,0:T(8,128)S(1)}, f32[1,7,160,128]{3,2,1,0:T(8,128)S(1)}, s32[1,16]{1,0:T(1,128)S...) while((s32[]{:T(128)}, f32[1,7,160]{2,1,0:T(8,128)S(1)}, ...), condition=%wide.region_9.10_spmd.clone, body=%wide.region_2.9_spmd.clone.sunk | while | flops 301698496 | bytes 8996831 | solution.py:95
  236.4 0.8 fusion.134
  237.9 3.4 conditional.9
  237.9 1.5 fusion.6
  239.4 1.0 fusion.9
  240.4 0.9 fusion.8
  242.7 0.8 fusion.134
  245.5 0.8 fusion.134
  248.3 0.8 fusion.134
  251.1 0.8 fusion.134
  253.9 0.8 fusion.134
  256.7 0.8 fusion.134
  259.5 0.8 fusion.134
  262.4 0.8 fusion.134
  265.2 0.8 fusion.134
  267.0 1.1 copy.53
  268.9 27.0 %all-to-all-start.1 = ((bf16[32,4,896]{2,1,0:T(4,128)(2,1)}), bf16[32,4,896]{2,1,0:T(4,128)(2,1)S(1)}, u32[]{:S(2)}, u32[]{:S(2)}) async-start(bf16[32,4,896]{2,1,0:T(4,128)(2,1)} %all_to_all.10), calls=%async_computation.1 | async-start | bytes 458752 | tf_op jit(solution)/shard_map/all_to_all | solution.py:238
  296.0 3.0 fusion.121
  299.0 5.4 %all-to-all-done.1 = bf16[32,4,896]{2,1,0:T(4,128)(2,1)S(1)} async-done(((bf16[32,4,896]{2,1,0:T(4,128)(2,1)}), bf16[32,4,896]{2,1,0:T(4,128)(2,1)S(1)}, u32[]{:S(2)}, u32[]{:S(2)}) %all-to-all-start.1) | async-done | bytes 229408 | tf_op jit(solution)/shard_map/all_to_all | solution.py:238
  305.7 39.6 %while.54 = (s32[]{:T(128)}, f32[160,1,7,128]{3,0,2,1:T(8,128)S(1)}, bf16[10,512,256]{1,2,0:T(8,128)(2,1)}, s32[1,16]{1,0:T(1,128)S(1)}, s32[10]{0:T(128)S(1)}, ...) while((s32[]{:T(128)}, ...), condition=%wide.region_27.28_spmd.clone, body=%wide.region_22.27_spmd.clone.sunk | while | flops 741032128 | bytes 14592339 | solution.py:178
  307.1 0.8 fusion.136
  308.5 4.0 conditional.11
  309.0 1.8 fusion.53
  314.6 0.8 fusion.136
  318.2 0.8 fusion.136
  321.7 0.8 fusion.136
  325.3 0.8 fusion.136
  328.8 0.8 fusion.136
  332.4 0.8 fusion.136
  336.0 0.8 fusion.136
  339.5 0.8 fusion.136
  343.1 0.8 fusion.136
  345.3 4.4 copy.49
  350.7 104.7 %reduce-scatter.5.cloned.1.call-done = bf16[160,256]{1,0:T(8,128)(2,1)} async-done(((bf16[5120,256]{1,0:T(8,128)(2,1)}), bf16[160,256]{1,0:T(8,128)(2,1)}) %reduce-scatter.5.cloned.1.call-update) | async-done | bytes 81936 | tf_op jit(solution)/shard_map/reduce_scatter | solution.py:282
  455.3 1.4 fusion.122
  (240 shorter events, 41.1 us)
Async XLA Ops:
  7.2 50.0 %all-gather.9.cloned.1.call-start = ((), (), s32[]{:S(2)}) async-start(), calls=%async_computation.6 | async-start | bytes 2703360 | tf_op jit(solution)/shard_map/all_gather | solution.py:212
  7.9 95.3 %all-gather.11.cloned.1.call-start = ((), (), s32[]{:S(2)}) async-start(), calls=%async_computation.7 | async-start | bytes 2703360 | tf_op jit(solution)/shard_map/all_gather | solution.py:213
  8.6 226.4 %all-gather.7.cloned.1.call-start = ((), (), s32[]{:S(2)}) async-start(), calls=%async_computation.5 | async-start | bytes 1351680 | tf_op jit(solution)/shard_map/all_gather | solution.py:219
  9.4 257.7 %reduce-scatter.7.cloned.1.call-start = ((), (), s32[]{:S(2)}) async-start(), calls=%async_computation.9 | async-start | bytes 1146880
  152.2 1.4 copy-start.2
  153.5 61.2 %copy-start.1 = (bf16[160,128]{1,0:T(8,128)(2,1)S(1)}, bf16[160,128]{1,0:T(8,128)(2,1)}, u32[]{:S(2)}) copy-start(bf16[160,128]{1,0:T(8,128)(2,1)} %param.28) | copy-start | bytes 122884
  153.6 61.8 %copy-start = (bf16[160,896]{1,0:T(8,128)(2,1)S(1)}, bf16[160,896]{1,0:T(8,128)(2,1)}, u32[]{:S(2)}) copy-start(bf16[160,896]{1,0:T(8,128)(2,1)} %param.27) | copy-start | bytes 860164
  154.8 61.0 %copy-start.3 = (s32[1,2,128]{2,1,0:T(2,128)S(1)}, s32[1,2,128]{2,1,0:T(2,128)}, u32[]{:S(2)}) copy-start(s32[1,2,128]{2,1,0:T(2,128)} %param.33) | copy-start | bytes 3076
  154.8 80.2 %all-to-all-start = ((bf16[32,160,128]{2,1,0:T(8,128)(2,1)}), bf16[32,160,128]{2,1,0:T(8,128)(2,1)S(1)}, u32[]{:S(2)}, u32[]{:S(2)}) async-start(bf16[32,160,128]{2,1,0:T(8,128)(2,1)} %stack.2), calls=%async_computation | async-start | bytes 2621440 | tf_op jit(solution)/shard_map/all_to_all | solution.py:221
  214.5 81.5 %all-gather.5.cloned.1.call-start = ((), (), s32[]{:S(2)}) async-start(), calls=%async_computation.4 | async-start | bytes 2703360 | tf_op jit(solution)/shard_map/all_gather | solution.py:16
  268.9 35.4 %all-to-all-start.1 = ((bf16[32,4,896]{2,1,0:T(4,128)(2,1)}), bf16[32,4,896]{2,1,0:T(4,128)(2,1)S(1)}, u32[]{:S(2)}, u32[]{:S(2)}) async-start(bf16[32,4,896]{2,1,0:T(4,128)(2,1)} %all_to_all.10), calls=%async_computation.1 | async-start | bytes 458752 | tf_op jit(solution)/shard_map/all_to_all | solution.py:238
  295.9 159.4 %reduce-scatter.5.cloned.1.call-start = ((), (), s32[]{:S(2)}) async-start(), calls=%async_computation.8 | async-start | bytes 2703360 | tf_op jit(solution)/shard_map/reduce_scatter | solution.py:282
Sparse Core Ops, SparseCore 0:
  10.2 46.9 all-gather.8
  59.5 43.7 all-gather.10
  105.5 42.1 all-gather.6
  153.7 76.7 reduce-scatter.6
  232.5 44.2 all-gather.4
  349.8 105.4 reduce-scatter.4
